TPU v7x, 32 devices: a whole 2x2x4 slice. The times are simulated.
32 devices in a mesh: cell: 8 (over z, y), inst: 4 (over x, core).
Axes of the slice: x: 2, y: 2, z: 4, core: 2. Of those that a mesh axis runs over, the one named last changes fastest.
Arguments:
- fine_residual: float32 [8, 6, 65536], P('inst', None, 'cell'), may hold values from -6 to 6
- fine_map: int32 [65536], P('cell'), may hold values from 0 to 15
- routes: int32 [8, 64], P('cell'), may hold values from 0 to 7, as said below
- receive_lists: int32 [8, 192], P('cell'), may hold values from 0 to 1023
- neighbours: int32 [6, 8192], P(None, 'cell'), may hold values from 0 to 1215, as said below
- face_weights: float32 [6, 8192], P(None, 'cell'), may hold values from 0.3 to 3
- spectral_coef: float32 [8192], P('cell'), may hold values from 0.2 to 1
- diag_extra: float32 [6, 8192], P(None, 'cell'), may hold values from 0.5 to 2
Outputs:
- fine_correction: float32 [8, 6, 65536], P('inst', None, 'cell')
- coarse_correction: float32 [8, 6, 8192], P('inst', None, 'cell')
Inputs may be any that keep to these rules, and one draw needn't show every extreme that they name: `routes`: in row p, the value p appears 64 - 2 * 4 times, and (p - 1) mod 8 and (p + 1) mod 8 appear 4 times each. `receive_lists`: row o, entries t * 32 to t * 32 + 31, list cells that partition o receives as halo from partition (o + d) mod 8, with d = t - 3 for t < 3 and d = t - 2 otherwise. `neighbours`: A value below 1024 is a cell of the own partition; a value x of 1024 or more is halo slot x - 1024.
All inputs are finite; a program needn't handle non-finite values.
Results may differ from a plain program's by a relative error of at most 0.0001.
Values sent between devices are 32-bit elements; how exact they have to be, the bound alone decides.
A program may use at most 64 MiB of HBM per device.

v0:
```python
import jax
import jax.numpy as jnp
from jax import lax
from jax.sharding import PartitionSpec as P

INST = 8
HB_INST = 7
NB = 6
AGG = 8
BLK = 128
RAD = 3
ITERS = 6


exact_precision = lax.Precision.HIGHEST


def shifted(value, axis, steps):
    count = lax.axis_size(axis)
    pairs = [(source, (source + steps) % count) for source in range(count)]
    return lax.ppermute(value, axis, pairs)


def spectral_matrix():
    row_ids = jnp.arange(INST)[:, None]
    col_ids = jnp.arange(INST)[None, :]
    distance = row_ids - col_ids
    usable = (row_ids < HB_INST) & (col_ids < HB_INST) & (distance != 0)
    parity = 1.0 - 2.0 * jnp.mod(distance, 2).astype(jnp.float32)
    denominator = jnp.sin(jnp.pi * jnp.where(usable, distance, 1).astype(jnp.float32) / HB_INST)
    return jnp.where(usable, 0.5 * parity / denominator, 0.0)


def body(
    fine_residual,
    fine_map,
    routes,
    receive_lists,
    neighbours,
    face_weights,
    spectral_coef,
    diag_extra,
):
    n_cell = lax.axis_size("cell")
    cell_index = lax.axis_index("cell")
    inst_index = lax.axis_index("inst")
    inst_dev, var_count, fine_dev = fine_residual.shape
    blocks = routes.shape[1]
    handed = blocks // 16
    coarse_block = BLK // AGG
    coarse_dev = blocks * coarse_block
    peer_slots = 2 * RAD
    halo_width = receive_lists.shape[1] // peer_slots
    offsets = [slot - RAD if slot < RAD else slot - RAD + 1 for slot in range(peer_slots)]
    relative = jnp.mod(routes[0] - cell_index, n_cell)
    category = jnp.where(relative == 1, 0, jnp.where(relative == 0, 1, 2)).astype(jnp.int32)
    block_ids = jnp.arange(blocks, dtype=jnp.int32)
    lower_class = jnp.sum((category[None, :] < category[:, None]).astype(jnp.int32), axis=1)
    same_before = (category[None, :] == category[:, None]) & (
        block_ids[None, :] < block_ids[:, None]
    )
    position = lower_class + jnp.sum(same_before.astype(jnp.int32), axis=1)
    permuter = (position[:, None] == block_ids[None, :]).astype(jnp.float32)
    cell_map = fine_map.reshape(blocks, BLK)
    one_hot = (
        cell_map[:, :, None] == jnp.arange(coarse_block, dtype=jnp.int32)[None, None, :]
    ).astype(jnp.float32)
    fine_blocks = fine_residual.reshape(inst_dev, var_count, blocks, BLK)
    restricted = jnp.einsum("ivbf,bfc->ivbc", fine_blocks, one_hot, precision=exact_precision)
    ordered = jnp.einsum("ivbc,bq->ivqc", restricted, permuter, precision=exact_precision)
    from_below = shifted(ordered[:, :, :handed], "cell", 1)
    from_above = shifted(ordered[:, :, blocks - handed :], "cell", -1)
    arrived = jnp.concatenate(
        [from_below, ordered[:, :, handed : blocks - handed], from_above], axis=2
    )
    arrived = arrived.reshape(inst_dev, var_count, coarse_dev)
    inst_ids = inst_index * inst_dev + jnp.arange(inst_dev)
    coarse_residual = jnp.where((inst_ids < HB_INST)[:, None, None], arrived, jnp.float32(0.0))
    own_lists = receive_lists[0].reshape(peer_slots, halo_width)
    send_lists = []
    for slot in range(peer_slots):
        send_lists.append(shifted(own_lists[slot], "cell", offsets[slot]))
    all_sends = jnp.concatenate(send_lists, axis=0)
    diagonal = jnp.sum(face_weights, axis=0)[None, :] + 3.0 * spectral_coef[None, :] + diag_extra
    spec_rows = spectral_matrix()[inst_ids]
    correction = coarse_residual / diagonal[None]
    for sweep in range(ITERS):
        outgoing = jnp.take(correction, all_sends, axis=2)
        pieces = []
        for halo_slot in range(peer_slots):
            values = outgoing[:, :, halo_slot * halo_width : (halo_slot + 1) * halo_width]
            pieces.append(shifted(values, "cell", -offsets[halo_slot]))
        extended = jnp.concatenate([correction, jnp.concatenate(pieces, axis=2)], axis=2)
        total = jnp.zeros_like(correction)
        for slot_index in range(NB):
            total = total + face_weights[slot_index][None, None, :] * jnp.take(
                extended, neighbours[slot_index], axis=2
            )
        gathered = lax.all_gather(correction, "inst", axis=0, tiled=True)
        summed = jnp.einsum("nm,mvc->nvc", spec_rows, gathered, precision=exact_precision)
        correction = (coarse_residual + total - spectral_coef[None, None, :] * summed) / diagonal[
            None
        ]
    coarse_blocks = correction.reshape(inst_dev, var_count, blocks, coarse_block)
    back_above = shifted(coarse_blocks[:, :, :handed], "cell", -1)
    back_below = shifted(coarse_blocks[:, :, blocks - handed :], "cell", 1)
    returned = jnp.concatenate(
        [back_above, coarse_blocks[:, :, handed : blocks - handed], back_below], axis=2
    )
    returned_blocks = jnp.einsum("ivqc,bq->ivbc", returned, permuter, precision=exact_precision)
    fine_correction = jnp.einsum(
        "ivbc,bfc->ivbf", returned_blocks, one_hot, precision=exact_precision
    )
    return (fine_correction.reshape(inst_dev, var_count, fine_dev), correction)


def solution(mesh):
    in_specs = (
        P("inst", None, "cell"),
        P("cell"),
        P("cell", None),
        P("cell", None),
        P(None, "cell"),
        P(None, "cell"),
        P("cell"),
        P(None, "cell"),
    )
    out_specs = (P("inst", None, "cell"), P("inst", None, "cell"))
    return jax.shard_map(body, mesh=mesh, in_specs=in_specs, out_specs=out_specs, check_vma=False)
```

profile of v0, /device:TPU:0, one launch (start us, length us, event | category | flops | bytes accessed | tf_op | source)
XLA Modules:
  0.0 390.8 jit_solution(1031421473719623911)
XLA Ops:
  78.7 6.4 %all_gather.19 = f32[8,6,1024]{2,1,0:T(8,128)} all-gather(f32[2,6,1024]{2,1,0:T(8,128)S(1)} %copy.233), channel_id=1, replica_groups=mesh['cell'=8,'inst'=4] {'inst'}, dimensions={0}, use_global_device_ids=true | all-gather | bytes 245760 | tf_op jit(solution)/shard_map/all_gather | solution.py:99
  86.3 7.6 %gather_fusion.9 = f32[1024,2,6]{2,1,0:T(2,128)} fusion(f32[2,6,1216]{1,0,2:T(2,128)S(1)} %copy.221, s32[1024]{0:T(1024)S(1)} %fusion.89), kind=kCustom, calls=%fused_computation.12.clone | custom fusion | bytes 102400 | tf_op jit(solution)/shard_map/jit(_take)/gather | solution.py:96
  93.9 7.5 %gather_fusion.10 = f32[1024,2,6]{2,1,0:T(2,128)} fusion(f32[2,6,1216]{1,0,2:T(2,128)S(1)} %copy.221, s32[1024]{0:T(1024)S(1)} %fusion.84), kind=kCustom, calls=%fused_computation.13.clone | custom fusion | bytes 102400 | tf_op jit(solution)/shard_map/jit(_take)/gather | solution.py:96
  101.4 7.5 %gather_fusion.11 = f32[1024,2,6]{2,1,0:T(2,128)} fusion(f32[2,6,1216]{1,0,2:T(2,128)S(1)} %copy.221, s32[1024]{0:T(1024)S(1)} %fusion.85), kind=kCustom, calls=%fused_computation.14.clone | custom fusion | bytes 102400 | tf_op jit(solution)/shard_map/jit(_take)/gather | solution.py:96
  109.0 7.5 %gather_fusion.12 = f32[1024,2,6]{2,1,0:T(2,128)} fusion(f32[2,6,1216]{1,0,2:T(2,128)S(1)} %copy.221, s32[1024]{0:T(1024)S(1)} %fusion.86), kind=kCustom, calls=%fused_computation.15.clone | custom fusion | bytes 102400 | tf_op jit(solution)/shard_map/jit(_take)/gather | solution.py:96
  141.6 6.2 %all_gather.20 = f32[8,6,1024]{2,1,0:T(8,128)} all-gather(f32[2,6,1024]{2,1,0:T(8,128)S(1)} %copy.249), channel_id=1, replica_groups=mesh['cell'=8,'inst'=4] {'inst'}, dimensions={0}, use_global_device_ids=true | all-gather | bytes 245760 | tf_op jit(solution)/shard_map/all_gather | solution.py:99
  149.1 7.6 %gather_fusion.16 = f32[1024,2,6]{2,1,0:T(2,128)} fusion(f32[2,6,1216]{1,0,2:T(2,128)S(1)} %copy.237, s32[1024]{0:T(1024)S(1)} %fusion.89), kind=kCustom, calls=%fused_computation.18.clone | custom fusion | bytes 102400 | tf_op jit(solution)/shard_map/jit(_take)/gather | solution.py:96
  156.7 7.5 %gather_fusion.17 = f32[1024,2,6]{2,1,0:T(2,128)} fusion(f32[2,6,1216]{1,0,2:T(2,128)S(1)} %copy.237, s32[1024]{0:T(1024)S(1)} %fusion.84), kind=kCustom, calls=%fused_computation.19.clone | custom fusion | bytes 102400 | tf_op jit(solution)/shard_map/jit(_take)/gather | solution.py:96
  164.2 7.5 %gather_fusion.18 = f32[1024,2,6]{2,1,0:T(2,128)} fusion(f32[2,6,1216]{1,0,2:T(2,128)S(1)} %copy.237, s32[1024]{0:T(1024)S(1)} %fusion.85), kind=kCustom, calls=%fused_computation.20.clone | custom fusion | bytes 102400 | tf_op jit(solution)/shard_map/jit(_take)/gather | solution.py:96
  171.7 7.5 %gather_fusion.19 = f32[1024,2,6]{2,1,0:T(2,128)} fusion(f32[2,6,1216]{1,0,2:T(2,128)S(1)} %copy.237, s32[1024]{0:T(1024)S(1)} %fusion.86), kind=kCustom, calls=%fused_computation.21.clone | custom fusion | bytes 102400 | tf_op jit(solution)/shard_map/jit(_take)/gather | solution.py:96
  204.3 6.4 %all_gather.21 = f32[8,6,1024]{2,1,0:T(8,128)} all-gather(f32[2,6,1024]{2,1,0:T(8,128)S(1)} %copy.265), channel_id=1, replica_groups=mesh['cell'=8,'inst'=4] {'inst'}, dimensions={0}, use_global_device_ids=true | all-gather | bytes 245760 | tf_op jit(solution)/shard_map/all_gather | solution.py:99
  212.0 7.6 %gather_fusion.23 = f32[1024,2,6]{2,1,0:T(2,128)} fusion(f32[2,6,1216]{1,0,2:T(2,128)S(1)} %copy.253, s32[1024]{0:T(1024)S(1)} %fusion.89), kind=kCustom, calls=%fused_computation.24.clone | custom fusion | bytes 102400 | tf_op jit(solution)/shard_map/jit(_take)/gather | solution.py:96
  219.6 7.5 %gather_fusion.24 = f32[1024,2,6]{2,1,0:T(2,128)} fusion(f32[2,6,1216]{1,0,2:T(2,128)S(1)} %copy.253, s32[1024]{0:T(1024)S(1)} %fusion.84), kind=kCustom, calls=%fused_computation.25.clone | custom fusion | bytes 102400 | tf_op jit(solution)/shard_map/jit(_take)/gather | solution.py:96
  227.1 7.5 %gather_fusion.25 = f32[1024,2,6]{2,1,0:T(2,128)} fusion(f32[2,6,1216]{1,0,2:T(2,128)S(1)} %copy.253, s32[1024]{0:T(1024)S(1)} %fusion.85), kind=kCustom, calls=%fused_computation.26.clone | custom fusion | bytes 102400 | tf_op jit(solution)/shard_map/jit(_take)/gather | solution.py:96
  234.6 7.5 %gather_fusion.26 = f32[1024,2,6]{2,1,0:T(2,128)} fusion(f32[2,6,1216]{1,0,2:T(2,128)S(1)} %copy.253, s32[1024]{0:T(1024)S(1)} %fusion.86), kind=kCustom, calls=%fused_computation.27.clone | custom fusion | bytes 102400 | tf_op jit(solution)/shard_map/jit(_take)/gather | solution.py:96
  274.7 7.6 %gather_fusion.30 = f32[1024,2,6]{2,1,0:T(2,128)} fusion(f32[2,6,1216]{1,0,2:T(2,128)S(1)} %copy.269, s32[1024]{0:T(1024)S(1)} %fusion.89), kind=kCustom, calls=%fused_computation.30.clone | custom fusion | bytes 102400 | tf_op jit(solution)/shard_map/jit(_take)/gather | solution.py:96
  282.3 7.5 %gather_fusion.31 = f32[1024,2,6]{2,1,0:T(2,128)} fusion(f32[2,6,1216]{1,0,2:T(2,128)S(1)} %copy.269, s32[1024]{0:T(1024)S(1)} %fusion.84), kind=kCustom, calls=%fused_computation.31.clone | custom fusion | bytes 102400 | tf_op jit(solution)/shard_map/jit(_take)/gather | solution.py:96
  289.8 7.5 %gather_fusion.32 = f32[1024,2,6]{2,1,0:T(2,128)} fusion(f32[2,6,1216]{1,0,2:T(2,128)S(1)} %copy.269, s32[1024]{0:T(1024)S(1)} %fusion.85), kind=kCustom, calls=%fused_computation.32.clone | custom fusion | bytes 102400 | tf_op jit(solution)/shard_map/jit(_take)/gather | solution.py:96
  297.3 7.5 %gather_fusion.33 = f32[1024,2,6]{2,1,0:T(2,128)} fusion(f32[2,6,1216]{1,0,2:T(2,128)S(1)} %copy.269, s32[1024]{0:T(1024)S(1)} %fusion.86), kind=kCustom, calls=%fused_computation.33.clone | custom fusion | bytes 102400 | tf_op jit(solution)/shard_map/jit(_take)/gather | solution.py:96
  330.0 6.5 %all_gather.23 = f32[8,6,1024]{2,1,0:T(8,128)} all-gather(f32[2,6,1024]{2,1,0:T(8,128)S(1)} %copy.297), channel_id=1, replica_groups=mesh['cell'=8,'inst'=4] {'inst'}, dimensions={0}, use_global_device_ids=true | all-gather | bytes 245760 | tf_op jit(solution)/shard_map/all_gather | solution.py:99
  344.8 7.6 %gather_fusion.39 = f32[1024,2,6]{2,1,0:T(2,128)} fusion(f32[2,6,1216]{1,0,2:T(2,128)S(1)} %copy.285, s32[1024]{0:T(1024)S(1)} %fusion.85), kind=kCustom, calls=%fused_computation.38.clone | custom fusion | bytes 102400 | tf_op jit(solution)/shard_map/jit(_take)/gather | solution.py:96
  352.4 7.5 %gather_fusion.40 = f32[1024,2,6]{2,1,0:T(2,128)} fusion(f32[2,6,1216]{1,0,2:T(2,128)S(1)} %copy.285, s32[1024]{0:T(1024)S(1)} %fusion.86), kind=kCustom, calls=%fused_computation.39.clone | custom fusion | bytes 102400 | tf_op jit(solution)/shard_map/jit(_take)/gather | solution.py:96
  359.9 7.5 %gather_fusion.41 = f32[1024,2,6]{2,1,0:T(2,128)} fusion(f32[2,6,1216]{1,0,2:T(2,128)S(1)} %copy.285, s32[1024]{0:T(1024)S(1)} %fusion.87), kind=kCustom, calls=%fused_computation.40.clone | custom fusion | bytes 102400 | tf_op jit(solution)/shard_map/jit(_take)/gather | solution.py:96
  367.5 7.5 %gather_fusion.42 = f32[1024,2,6]{2,1,0:T(2,128)} fusion(f32[2,6,1216]{1,0,2:T(2,128)S(1)} %copy.285, s32[1024]{0:T(1024)S(1)} %fusion.88), kind=kCustom, calls=%fused_computation.41.clone | custom fusion | bytes 102400 | tf_op jit(solution)/shard_map/jit(_take)/gather | solution.py:96
  (373 shorter events, 212.3 us)
Async XLA Ops:
  5.7 18.2 %collective-permute-start = (f32[2,6,4,16]{2,3,1,0:T(8,128)S(1)}, f32[2,6,4,16]{2,3,1,0:T(8,128)S(1)}, u32[]{:S(2)}, u32[]{:S(2)}) collective-permute-start(f32[2,6,4,16]{2,3,1,0:T(8,128)S(1)} %get-tuple-element.8), channel_id=1, source_target_pairs={{0,4},{4,8},{8,12},{12,16},{16,20},{20,24},{24,28},{28,0},{1,5},{5... | collective-permute-start | bytes 9224 | tf_op jit(solution)/shard_map/ppermute | solution.py:21
  8.7 15.1 %collective-permute-start.1 = (f32[2,6,4,16]{2,3,1,0:T(8,128)S(1)}, f32[2,6,4,16]{2,3,1,0:T(8,128)S(1)}, u32[]{:S(2)}, u32[]{:S(2)}) collective-permute-start(f32[2,6,4,16]{2,3,1,0:T(8,128)S(1)} %get-tuple-element.9), channel_id=1, source_target_pairs={{0,28},{4,0},{8,4},{12,8},{16,12},{20,16},{24,20},{28,24},{1,29},{... | collective-permute-start | bytes 9224 | tf_op jit(solution)/shard_map/ppermute | solution.py:21
  30.3 12.0 %collective-permute-start.11 = (f32[2,6,32]{2,0,1:T(2,128)S(1)}, f32[2,6,32]{2,0,1:T(2,128)S(1)}, u32[]{:S(2)}, u32[]{:S(2)}) collective-permute-start(f32[2,6,32]{2,0,1:T(2,128)S(1)} %get-tuple-element.54), channel_id=1, source_target_pairs={{0,28},{4,0},{8,4},{12,8},{16,12},{20,16},{24,20},{28,24},{1,29},{... | collective-permute-start | bytes 4616 | tf_op jit(solution)/shard_map/ppermute | solution.py:21
  31.6 10.7 %collective-permute-start.12 = (f32[2,6,32]{2,0,1:T(2,128)S(1)}, f32[2,6,32]{2,0,1:T(2,128)S(1)}, u32[]{:S(2)}, u32[]{:S(2)}) collective-permute-start(f32[2,6,32]{2,0,1:T(2,128)S(1)} %get-tuple-element.53), channel_id=1, source_target_pairs={{0,24},{4,28},{8,0},{12,4},{16,8},{20,12},{24,16},{28,20},{1,25},{... | collective-permute-start | bytes 4616 | tf_op jit(solution)/shard_map/ppermute | solution.py:21
  32.2 10.1 %collective-permute-start.13 = (f32[2,6,32]{2,0,1:T(2,128)S(1)}, f32[2,6,32]{2,0,1:T(2,128)S(1)}, u32[]{:S(2)}, u32[]{:S(2)}) collective-permute-start(f32[2,6,32]{2,0,1:T(2,128)S(1)} %get-tuple-element.52), channel_id=1, source_target_pairs={{0,20},{4,24},{8,28},{12,0},{16,4},{20,8},{24,12},{28,16},{1,21},{... | collective-permute-start | bytes 4616 | tf_op jit(solution)/shard_map/ppermute | solution.py:21
  71.3 13.8 %collective-permute-start.15 = (f32[2,6,32]{2,0,1:T(2,128)S(1)}, f32[2,6,32]{2,0,1:T(2,128)S(1)}, u32[]{:S(2)}, u32[]{:S(2)}) collective-permute-start(f32[2,6,32]{2,0,1:T(2,128)S(1)} %get-tuple-element.50), channel_id=1, source_target_pairs={{0,8},{4,12},{8,16},{12,20},{16,24},{20,28},{24,0},{28,4},{1,9},{5... | collective-permute-start | bytes 4616 | tf_op jit(solution)/shard_map/ppermute | solution.py:21
  71.7 13.4 %collective-permute-start.16 = (f32[2,6,32]{2,0,1:T(2,128)S(1)}, f32[2,6,32]{2,0,1:T(2,128)S(1)}, u32[]{:S(2)}, u32[]{:S(2)}) collective-permute-start(f32[2,6,32]{2,0,1:T(2,128)S(1)} %get-tuple-element.49), channel_id=1, source_target_pairs={{0,4},{4,8},{8,12},{12,16},{16,20},{20,24},{24,28},{28,0},{1,5},{5... | collective-permute-start | bytes 4616 | tf_op jit(solution)/shard_map/ppermute | solution.py:21
  74.6 10.4 %collective-permute-start.17 = (f32[2,6,32]{2,0,1:T(2,128)S(1)}, f32[2,6,32]{2,0,1:T(2,128)S(1)}, u32[]{:S(2)}, u32[]{:S(2)}) collective-permute-start(f32[2,6,32]{2,0,1:T(2,128)S(1)} %get-tuple-element.48), channel_id=1, source_target_pairs={{0,28},{4,0},{8,4},{12,8},{16,12},{20,16},{24,20},{28,24},{1,29},{... | collective-permute-start | bytes 4616 | tf_op jit(solution)/shard_map/ppermute | solution.py:21
  131.8 9.3 %collective-permute-start.20 = (f32[2,6,32]{2,0,1:T(2,128)S(1)}, f32[2,6,32]{2,0,1:T(2,128)S(1)}, u32[]{:S(2)}, u32[]{:S(2)}) collective-permute-start(f32[2,6,32]{2,0,1:T(2,128)S(1)} %get-tuple-element.45), channel_id=1, source_target_pairs={{0,12},{4,16},{8,20},{12,24},{16,28},{20,0},{24,4},{28,8},{1,13},{... | collective-permute-start | bytes 4616 | tf_op jit(solution)/shard_map/ppermute | solution.py:21
  134.3 13.5 %collective-permute-start.21 = (f32[2,6,32]{2,0,1:T(2,128)S(1)}, f32[2,6,32]{2,0,1:T(2,128)S(1)}, u32[]{:S(2)}, u32[]{:S(2)}) collective-permute-start(f32[2,6,32]{2,0,1:T(2,128)S(1)} %get-tuple-element.44), channel_id=1, source_target_pairs={{0,8},{4,12},{8,16},{12,20},{16,24},{20,28},{24,0},{28,4},{1,9},{5... | collective-permute-start | bytes 4616 | tf_op jit(solution)/shard_map/ppermute | solution.py:21
  135.4 12.4 %collective-permute-start.22 = (f32[2,6,32]{2,0,1:T(2,128)S(1)}, f32[2,6,32]{2,0,1:T(2,128)S(1)}, u32[]{:S(2)}, u32[]{:S(2)}) collective-permute-start(f32[2,6,32]{2,0,1:T(2,128)S(1)} %get-tuple-element.43), channel_id=1, source_target_pairs={{0,4},{4,8},{8,12},{12,16},{16,20},{20,24},{24,28},{28,0},{1,5},{5... | collective-permute-start | bytes 4616 | tf_op jit(solution)/shard_map/ppermute | solution.py:21
  137.0 10.8 %collective-permute-start.23 = (f32[2,6,32]{2,0,1:T(2,128)S(1)}, f32[2,6,32]{2,0,1:T(2,128)S(1)}, u32[]{:S(2)}, u32[]{:S(2)}) collective-permute-start(f32[2,6,32]{2,0,1:T(2,128)S(1)} %get-tuple-element.42), channel_id=1, source_target_pairs={{0,28},{4,0},{8,4},{12,8},{16,12},{20,16},{24,20},{28,24},{1,29},{... | collective-permute-start | bytes 4616 | tf_op jit(solution)/shard_map/ppermute | solution.py:21
  194.5 9.3 %collective-permute-start.26 = (f32[2,6,32]{2,0,1:T(2,128)S(1)}, f32[2,6,32]{2,0,1:T(2,128)S(1)}, u32[]{:S(2)}, u32[]{:S(2)}) collective-permute-start(f32[2,6,32]{2,0,1:T(2,128)S(1)} %get-tuple-element.39), channel_id=1, source_target_pairs={{0,12},{4,16},{8,20},{12,24},{16,28},{20,0},{24,4},{28,8},{1,13},{... | collective-permute-start | bytes 4616 | tf_op jit(solution)/shard_map/ppermute | solution.py:21
  197.0 13.8 %collective-permute-start.27 = (f32[2,6,32]{2,0,1:T(2,128)S(1)}, f32[2,6,32]{2,0,1:T(2,128)S(1)}, u32[]{:S(2)}, u32[]{:S(2)}) collective-permute-start(f32[2,6,32]{2,0,1:T(2,128)S(1)} %get-tuple-element.38), channel_id=1, source_target_pairs={{0,8},{4,12},{8,16},{12,20},{16,24},{20,28},{24,0},{28,4},{1,9},{5... | collective-permute-start | bytes 4616 | tf_op jit(solution)/shard_map/ppermute | solution.py:21
  198.1 12.6 %collective-permute-start.28 = (f32[2,6,32]{2,0,1:T(2,128)S(1)}, f32[2,6,32]{2,0,1:T(2,128)S(1)}, u32[]{:S(2)}, u32[]{:S(2)}) collective-permute-start(f32[2,6,32]{2,0,1:T(2,128)S(1)} %get-tuple-element.37), channel_id=1, source_target_pairs={{0,4},{4,8},{8,12},{12,16},{16,20},{20,24},{24,28},{28,0},{1,5},{5... | collective-permute-start | bytes 4616 | tf_op jit(solution)/shard_map/ppermute | solution.py:21
  199.7 11.1 %collective-permute-start.29 = (f32[2,6,32]{2,0,1:T(2,128)S(1)}, f32[2,6,32]{2,0,1:T(2,128)S(1)}, u32[]{:S(2)}, u32[]{:S(2)}) collective-permute-start(f32[2,6,32]{2,0,1:T(2,128)S(1)} %get-tuple-element.36), channel_id=1, source_target_pairs={{0,28},{4,0},{8,4},{12,8},{16,12},{20,16},{24,20},{28,24},{1,29},{... | collective-permute-start | bytes 4616 | tf_op jit(solution)/shard_map/ppermute | solution.py:21
  257.4 9.3 %collective-permute-start.32 = (f32[2,6,32]{2,0,1:T(2,128)S(1)}, f32[2,6,32]{2,0,1:T(2,128)S(1)}, u32[]{:S(2)}, u32[]{:S(2)}) collective-permute-start(f32[2,6,32]{2,0,1:T(2,128)S(1)} %get-tuple-element.33), channel_id=1, source_target_pairs={{0,12},{4,16},{8,20},{12,24},{16,28},{20,0},{24,4},{28,8},{1,13},{... | collective-permute-start | bytes 4616 | tf_op jit(solution)/shard_map/ppermute | solution.py:21
  259.9 13.5 %collective-permute-start.33 = (f32[2,6,32]{2,0,1:T(2,128)S(1)}, f32[2,6,32]{2,0,1:T(2,128)S(1)}, u32[]{:S(2)}, u32[]{:S(2)}) collective-permute-start(f32[2,6,32]{2,0,1:T(2,128)S(1)} %get-tuple-element.32), channel_id=1, source_target_pairs={{0,8},{4,12},{8,16},{12,20},{16,24},{20,28},{24,0},{28,4},{1,9},{5... | collective-permute-start | bytes 4616 | tf_op jit(solution)/shard_map/ppermute | solution.py:21
  261.0 12.4 %collective-permute-start.34 = (f32[2,6,32]{2,0,1:T(2,128)S(1)}, f32[2,6,32]{2,0,1:T(2,128)S(1)}, u32[]{:S(2)}, u32[]{:S(2)}) collective-permute-start(f32[2,6,32]{2,0,1:T(2,128)S(1)} %get-tuple-element.31), channel_id=1, source_target_pairs={{0,4},{4,8},{8,12},{12,16},{16,20},{20,24},{24,28},{28,0},{1,5},{5... | collective-permute-start | bytes 4616 | tf_op jit(solution)/shard_map/ppermute | solution.py:21
  262.6 10.8 %collective-permute-start.35 = (f32[2,6,32]{2,0,1:T(2,128)S(1)}, f32[2,6,32]{2,0,1:T(2,128)S(1)}, u32[]{:S(2)}, u32[]{:S(2)}) collective-permute-start(f32[2,6,32]{2,0,1:T(2,128)S(1)} %get-tuple-element.30), channel_id=1, source_target_pairs={{0,28},{4,0},{8,4},{12,8},{16,12},{20,16},{24,20},{28,24},{1,29},{... | collective-permute-start | bytes 4616 | tf_op jit(solution)/shard_map/ppermute | solution.py:21
  320.1 9.3 %collective-permute-start.38 = (f32[2,6,32]{2,0,1:T(2,128)S(1)}, f32[2,6,32]{2,0,1:T(2,128)S(1)}, u32[]{:S(2)}, u32[]{:S(2)}) collective-permute-start(f32[2,6,32]{2,0,1:T(2,128)S(1)} %get-tuple-element.27), channel_id=1, source_target_pairs={{0,12},{4,16},{8,20},{12,24},{16,28},{20,0},{24,4},{28,8},{1,13},{... | collective-permute-start | bytes 4616 | tf_op jit(solution)/shard_map/ppermute | solution.py:21
  322.7 13.8 %collective-permute-start.39 = (f32[2,6,32]{2,0,1:T(2,128)S(1)}, f32[2,6,32]{2,0,1:T(2,128)S(1)}, u32[]{:S(2)}, u32[]{:S(2)}) collective-permute-start(f32[2,6,32]{2,0,1:T(2,128)S(1)} %get-tuple-element.26), channel_id=1, source_target_pairs={{0,8},{4,12},{8,16},{12,20},{16,24},{20,28},{24,0},{28,4},{1,9},{5... | collective-permute-start | bytes 4616 | tf_op jit(solution)/shard_map/ppermute | solution.py:21
  323.8 12.6 %collective-permute-start.40 = (f32[2,6,32]{2,0,1:T(2,128)S(1)}, f32[2,6,32]{2,0,1:T(2,128)S(1)}, u32[]{:S(2)}, u32[]{:S(2)}) collective-permute-start(f32[2,6,32]{2,0,1:T(2,128)S(1)} %get-tuple-element.25), channel_id=1, source_target_pairs={{0,4},{4,8},{8,12},{12,16},{16,20},{20,24},{24,28},{28,0},{1,5},{5... | collective-permute-start | bytes 4616 | tf_op jit(solution)/shard_map/ppermute | solution.py:21
  325.4 11.1 %collective-permute-start.41 = (f32[2,6,32]{2,0,1:T(2,128)S(1)}, f32[2,6,32]{2,0,1:T(2,128)S(1)}, u32[]{:S(2)}, u32[]{:S(2)}) collective-permute-start(f32[2,6,32]{2,0,1:T(2,128)S(1)} %get-tuple-element.24), channel_id=1, source_target_pairs={{0,28},{4,0},{8,4},{12,8},{16,12},{20,16},{24,20},{28,24},{1,29},{... | collective-permute-start | bytes 4616 | tf_op jit(solution)/shard_map/ppermute | solution.py:21
  (84 other events, 2962.9 us)
where the time goes:
time: 391 us
  local copies, waits for them, and re-layouts  259 us (66%)
  starting transfers between devices  76.2 us (19%)
  blocking collectives  37.5 us (10%)
  waiting for transfers between devices  7.43 us (2%)
  matrix products  6.04 us (2%)
    gather x72, local copies, waits for them, and re-layouts, body(): jnp.take(extended, neighbours[slot_index], axis=2)  236 us
    ppermute x46, starting transfers between devices, shifted(): return lax.ppermute(value, axis, pairs)  76.2 us
    all_gather x6, blocking collectives, body(): gathered = lax.all_gather(correction, 'inst', axis=0, tiled=True)  37.5 us
  transfers between devices with their start and end apart: 46, of which 5 were waited for; matrix products, arithmetic and copies ran while one was open for 0% of the time, Pallas kernels for 0%

commit v1 on v0

v1 whole, which is shorter than its diff:
```python
import functools
import math

import jax
import jax.numpy as jnp
from jax import lax
from jax.experimental import pallas as pl
from jax.experimental.pallas import tpu as pltpu
from jax.sharding import PartitionSpec as P

INST = 8
HB_INST = 7
AGG = 8
BLK = 128
RAD = 3
ITERS = 6
LANES = 128
MESH = pl.DeviceIdType.MESH
CBLK = BLK // AGG
PER_TILE = LANES // CBLK

OFFSETS = [slot - RAD if slot < RAD else slot - RAD + 1 for slot in range(2 * RAD)]
NN = (((1,), (0,)), ((), ()))
NT = (((1,), (1,)), ((), ()))


def dot(a, b, dims=NN):
    return lax.dot_general(a, b, dims, preferred_element_type=jnp.float32)


def split(x):
    hi = x.astype(jnp.bfloat16)
    return hi, (x - hi.astype(jnp.float32)).astype(jnp.bfloat16)


def stack(x):
    return jnp.concatenate(split(x), axis=0)


def fold(y):
    half = y.shape[0] // 2
    return y[:half] + y[half:]


def iota(shape, dim):
    return lax.broadcasted_iota(jnp.int32, shape, dim)


def as_bf16(mask):
    return jnp.where(mask, 1.0, 0.0).astype(jnp.bfloat16)


def spectral_block(rows):
    shape = (rows, 3 * rows)
    row, col = iota(shape, 0), iota(shape, 1)
    part, m = col // rows, col % rows
    same = (row // INST == m // INST) & (row % INST < HB_INST) & (m % INST < HB_INST)
    dist = row % INST - m % INST
    full = jnp.zeros(shape, jnp.float32)
    for d in range(1 - HB_INST, HB_INST):
        if d:
            value = 0.5 * (-1.0) ** d / math.sin(math.pi * d / HB_INST)
            full = jnp.where(same & (dist == d), jnp.float32(value), full)
    hi, lo = split(full)
    return jnp.where(part < 2, hi.astype(jnp.float32), lo.astype(jnp.float32)).astype(jnp.bfloat16)


def kernel(
    n_cell, n_inst, vpd,
    fine_ref, map_ref, routes_ref, lists_ref, nb_ref, w_ref, sc_ref, de_ref,
    fine_out, coarse_out,
    e_ref, q_ref, ahi, alo, s_ref,
    sbuf, rbuf, rlo, rhi, lbuf, obuf, hbuf, fbuf, gbuf, glo, ghi,
    a_send, a_recv, l_send, l_recv, h_send, h_recv, f_send, f_recv,
):
    inst_dev, n_var, _ = fine_ref.shape
    coarse = nb_ref.shape[1]
    blocks = routes_ref.shape[1]
    hw = lists_ref.shape[1] // (2 * RAD)
    per = LANES // hw
    n_halo = s_ref.shape[1]
    halo_tiles = n_halo // LANES
    handed = blocks // 16 * CBLK
    groups = blocks // PER_TILE
    span = PER_TILE * BLK
    pad_var = vpd * n_inst
    rows = vpd * INST
    cell = lax.axis_index("cell")
    me = lax.axis_index("inst")

    def at(dc, inst):
        return {"cell": lax.rem(cell + (dc + n_cell), n_cell), "inst": inst}

    def other(k):
        return lax.rem(me + k, n_inst)

    barrier = pltpu.get_barrier_semaphore()
    greeted = [(d, 0) for d in OFFSETS]
    greeted += [(d, k) for d in (-1, 0, 1) for k in range(n_inst) if k]
    for d, k in greeted:
        pl.semaphore_signal(barrier, inc=1, device_id=at(d, other(k)), device_id_type=MESH)

    lane = iota((1, span), 1)
    sub = iota((LANES, span), 0)
    parts = []
    for g in range(groups):
        want = map_ref[:, g * span:(g + 1) * span] + (lane // BLK) * CBLK
        e_ref[g] = as_bf16(sub == want)
        x = fine_ref[:, :, g * span:(g + 1) * span]
        pieces = []
        for i in range(inst_dev):
            pieces.append(x[i])
            if pad_var > n_var:
                pieces.append(jnp.zeros((pad_var - n_var, span), jnp.float32))
        x = jnp.concatenate(pieces, axis=0)
        parts.append(fold(dot(stack(x), e_ref[g], NT)))
    y = jnp.concatenate(parts, axis=1)

    rel = lax.rem(routes_ref[...] - cell + n_cell, n_cell)
    kinds = [(rel == 1), (rel == 0), (rel != 1) & (rel != 0)]
    ind = [jnp.where(k, 1.0, 0.0) for k in kinds]
    tri = as_bf16(iota((blocks, blocks), 0) < iota((blocks, blocks), 1))
    pos = jnp.zeros((1, blocks), jnp.float32)
    base = jnp.zeros((1, 1), jnp.float32)
    for k in ind:
        before = dot(jnp.broadcast_to(k, (16, blocks)).astype(jnp.bfloat16), tri)[:1]
        pos = pos + k * (before + base)
        base = base + jnp.sum(k, axis=1, keepdims=True)
    rep = as_bf16(iota((blocks, coarse), 0) == iota((blocks, coarse), 1) // CBLK)
    pos = dot(jnp.broadcast_to(pos, (16, blocks)).astype(jnp.bfloat16), rep)[:1]
    target = pos.astype(jnp.int32) * CBLK + iota((1, coarse), 1) % CBLK
    q_ref[...] = as_bf16(iota((coarse, coarse), 0) == target)

    row = iota((inst_dev * pad_var, 1), 0)
    live = me * inst_dev + row // pad_var < HB_INST
    y = jnp.where(live, fold(dot(stack(y), q_ref[...], NT)), 0.0)
    for j in range(n_inst):
        picked = []
        for v in range(vpd):
            for i in range(inst_dev):
                r = i * pad_var + j * vpd + v
                picked.append(y[r:r + 1])
        sbuf[j] = jnp.concatenate(picked, axis=0)

    pl.semaphore_wait(barrier, len(greeted))

    def remote(src, dst, send, recv, dc, inst):
        copy = pltpu.make_async_remote_copy(
            src_ref=src, dst_ref=dst, send_sem=send, recv_sem=recv,
            device_id=at(dc, inst), device_id_type=MESH)
        copy.start()
        return copy

    def swap(src, mid, low, high, send, recv, dc):
        copies = []
        for k in range(n_inst):
            j = other(k)
            if k:
                copies.append(remote(src.at[j], mid.at[me], send.at[0, k], recv.at[0, k], 0, j))
            copies.append(remote(
                src.at[j, :, pl.ds(0, LANES)], low.at[me], send.at[1, k], recv.at[1, k], dc, j))
            copies.append(remote(
                src.at[j, :, pl.ds(coarse - LANES, LANES)], high.at[me],
                send.at[2, k], recv.at[2, k], -dc, j))
        mid[me] = src[me]
        return copies

    list_copies = [
        remote(lists_ref, lbuf.at[t], l_send.at[t], l_recv.at[t], OFFSETS[t], me)
        for t in range(2 * RAD)]
    swaps = swap(sbuf, rbuf, rlo, rhi, a_send, a_recv, 1)

    chunk = 64

    def build(k, carry):
        at_row = pl.multiple_of(k * chunk, chunk)
        ids = iota((chunk, coarse), 0) + k * chunk
        total = jnp.zeros((chunk, coarse), jnp.float32)
        for s in range(nb_ref.shape[0]):
            total = total + jnp.where(nb_ref[s:s + 1] == ids, w_ref[s:s + 1], 0.0)
        hi, lo = split(total)
        ahi[pl.ds(at_row, chunk)] = hi
        alo[pl.ds(at_row, chunk)] = lo
        return carry

    lax.fori_loop(0, (coarse + n_halo) // chunk, build, 0)

    sc = sc_ref[...]
    wsum = jnp.sum(w_ref[...], axis=0, keepdims=True) + 3.0 * sc
    diags = []
    for v in range(vpd):
        extra = jnp.zeros_like(sc)
        for var in range(n_var):
            extra = jnp.where(me * vpd + v == var, de_ref[var:var + 1], extra)
        diags.append(jnp.broadcast_to(wsum + extra, (INST, coarse)))
    rinv = 1.0 / jnp.concatenate(diags, axis=0)
    scr = sc * rinv
    spec = spectral_block(rows)

    lane = iota((1, LANES), 1)

    def pick(tile, get):
        value = get(tile * per)
        for t in range(tile * per + 1, min((tile + 1) * per, 2 * RAD)):
            value = jnp.where(lane // hw == t % per, get(t), value)
        return value

    for copy in list_copies:
        copy.wait()
    sub = iota((coarse, LANES), 0)
    for tile in range(halo_tiles):
        def listed(t):
            value = lbuf[t]
            width = value.shape[1]
            start = tile * LANES
            if start + LANES <= width:
                return value[:, start:start + LANES]
            return jnp.concatenate(
                [value[:, start:], jnp.zeros((1, start + LANES - width), jnp.int32)], axis=1)
        s_ref[:, tile * LANES:(tile + 1) * LANES] = as_bf16(sub == pick(tile, listed))

    for copy in swaps:
        copy.wait()
    wide = iota((1, coarse), 1)

    def edges(whole, low, high):
        fill = jnp.zeros((whole.shape[0], coarse - LANES), jnp.float32)
        low = jnp.concatenate([low, fill], axis=1)
        high = jnp.concatenate([fill, high], axis=1)
        return jnp.where(wide < handed, low, jnp.where(wide >= coarse - handed, high, whole))

    def ordered(buf):
        return jnp.concatenate(
            [buf[i, v * inst_dev:(v + 1) * inst_dev] for v in range(vpd) for i in range(n_inst)],
            axis=0)

    first = edges(ordered(rbuf), ordered(rlo), ordered(rhi)) * rinv

    def sweep(s, x):
        hi, lo = split(x)
        both = jnp.concatenate([hi, lo], axis=0)
        out = fold(dot(both, s_ref[...]))
        for tile in range(halo_tiles):
            obuf[s, tile] = out[:, tile * LANES:(tile + 1) * LANES]
        copies = [
            remote(obuf.at[s, t // per], hbuf.at[s, t], h_send.at[s, t], h_recv.at[s, t],
                   -OFFSETS[t], me)
            for t in range(2 * RAD)]
        total = fold(dot(both, ahi[:coarse])) + dot(hi, alo[:coarse])
        coupled = dot(spec, jnp.concatenate([hi, lo, hi], axis=0))
        partial = first + total * rinv - coupled * scr
        for copy in copies:
            copy.wait()
        halo = jnp.concatenate(
            [pick(tile, lambda t: hbuf[s, t]) for tile in range(halo_tiles)], axis=1)
        hi, lo = split(halo)
        both = jnp.concatenate([hi, lo], axis=0)
        return partial + rinv * (fold(dot(both, ahi[coarse:])) + dot(hi, alo[coarse:]))

    x = lax.fori_loop(0, ITERS, sweep, first)

    for i in range(n_inst):
        fbuf[i] = jnp.concatenate(
            [x[v * INST + i * inst_dev:v * INST + (i + 1) * inst_dev] for v in range(vpd)], axis=0)
    swaps = swap(fbuf, gbuf, glo, ghi, f_send, f_recv, -1)
    for copy in swaps:
        copy.wait()

    def by_var(buf):
        return jnp.concatenate(
            [buf[j, v * inst_dev + i:v * inst_dev + i + 1]
             for i in range(inst_dev) for j in range(n_inst) for v in range(vpd)], axis=0)

    whole = by_var(gbuf)
    for i in range(inst_dev):
        coarse_out[i] = whole[i * pad_var:i * pad_var + n_var]
    back = dot(stack(edges(whole, by_var(glo), by_var(ghi))), q_ref[...]).astype(jnp.bfloat16)
    for g in range(groups):
        fine = fold(dot(back[:, g * LANES:(g + 1) * LANES], e_ref[g]))
        for i in range(inst_dev):
            fine_out[i, :, g * span:(g + 1) * span] = fine[i * pad_var:i * pad_var + n_var]


def body(n_cell, n_inst, fine_residual, fine_map, routes, receive_lists, neighbours,
         face_weights, spectral_coef, diag_extra):
    inst_dev, n_var, fine_dev = fine_residual.shape
    coarse = neighbours.shape[1]
    blocks = routes.shape[1]
    halo = receive_lists.shape[1]
    n_halo = -(-halo // LANES) * LANES
    vpd = -(-n_var // n_inst)
    rows = vpd * INST
    part = vpd * inst_dev
    f32, bf16 = jnp.float32, jnp.bfloat16
    vmem = pl.BlockSpec(memory_space=pltpu.VMEM)
    dma = pltpu.SemaphoreType.DMA
    return pl.pallas_call(
        functools.partial(kernel, n_cell, n_inst, vpd),
        out_shape=(
            jax.ShapeDtypeStruct(fine_residual.shape, f32),
            jax.ShapeDtypeStruct((inst_dev, n_var, coarse), f32),
        ),
        in_specs=[vmem] * 8,
        out_specs=(vmem, vmem),
        scratch_shapes=[
            pltpu.VMEM((blocks // PER_TILE, LANES, PER_TILE * BLK), bf16),
            pltpu.VMEM((coarse, coarse), bf16),
            pltpu.VMEM((coarse + n_halo, coarse), bf16),
            pltpu.VMEM((coarse + n_halo, coarse), bf16),
            pltpu.VMEM((coarse, n_halo), bf16),
            pltpu.VMEM((n_inst, part, coarse), f32),
            pltpu.VMEM((n_inst, part, coarse), f32),
            pltpu.VMEM((n_inst, part, LANES), f32),
            pltpu.VMEM((n_inst, part, LANES), f32),
            pltpu.VMEM((2 * RAD, 1, halo), jnp.int32),
            pltpu.VMEM((ITERS, n_halo // LANES, rows, LANES), f32),
            pltpu.VMEM((ITERS, 2 * RAD, rows, LANES), f32),
            pltpu.VMEM((n_inst, part, coarse), f32),
            pltpu.VMEM((n_inst, part, coarse), f32),
            pltpu.VMEM((n_inst, part, LANES), f32),
            pltpu.VMEM((n_inst, part, LANES), f32),
            dma((3, n_inst)), dma((3, n_inst)),
            dma((2 * RAD,)), dma((2 * RAD,)),
            dma((ITERS, 2 * RAD)), dma((ITERS, 2 * RAD)),
            dma((3, n_inst)), dma((3, n_inst)),
        ],
        compiler_params=pltpu.CompilerParams(
            collective_id=0, has_side_effects=True, vmem_limit_bytes=48 * 1024 * 1024),
        name="multigrid",
    )(fine_residual, fine_map.reshape(1, -1), routes, receive_lists, neighbours,
      face_weights, spectral_coef.reshape(1, -1), diag_extra)


def solution(mesh):
    in_specs = (
        P("inst", None, "cell"),
        P("cell"),
        P("cell", None),
        P("cell", None),
        P(None, "cell"),
        P(None, "cell"),
        P("cell"),
        P(None, "cell"),
    )
    out_specs = (P("inst", None, "cell"), P("inst", None, "cell"))
    run = functools.partial(body, mesh.shape["cell"], mesh.shape["inst"])
    return jax.shard_map(run, mesh=mesh, in_specs=in_specs, out_specs=out_specs, check_vma=False)
```

time: 391 us -> 50.9 us (0.13)
  local copies, waits for them, and re-layouts: 259 us -> 3.01 us
  starting transfers between devices: 76.2 us -> 0 us
  Pallas kernels: 0 us -> 47 us
  blocking collectives: 37.5 us -> 0 us
  waiting for transfers between devices: 7.43 us -> 0 us
  matrix products: 6.04 us -> 0 us
    gather x85 -> x0, local copies, waits for them, and re-layouts: 243 us -> none  [the longest x72 236 us: body(): jnp.take(extended, neighbours[slot_index], axis=2)]
    ppermute x46 -> x0, starting transfers between devices: 76.2 us -> none  [shifted(): return lax.ppermute(value, axis, pairs)]
    pallas_call x0 -> x1, Pallas kernels: none -> 47 us  [body(): pl.pallas_call(functools.partial(kernel, n_cell, n_inst, vpd), out_shape=...]
    all_gather x6 -> x0, blocking collectives: 37.5 us -> none  [body(): gathered = lax.all_gather(correction, 'inst', axis=0, tiled=True)]
    concatenate x14 -> x0, local copies, waits for them, and re-layouts: 7.67 us -> none  [the longest x12 7.42 us: body(): jnp.concatenate([correction, jnp.concatenate(pieces, axis=2)], axis=2)]
    ppermute x46 -> x0, waiting for transfers between devices: 7.43 us -> none  [shifted(): return lax.ppermute(value, axis, pairs)]
    dot_general x10 -> x0, matrix products: 6.04 us -> none  [the longest x6 3.33 us: body(): jnp.einsum('nm,mvc->nvc', spec_rows, gathered, precision=exact_precision)]
  transfers between devices with their start and end apart: 46 -> 0, of which waited for: 5 -> 0; matrix products, arithmetic and copies ran while one was open for 0% -> 0% of each run, Pallas kernels for 0% -> 0%
where the time goes in v1:
time: 50.9 us; the launch traced here: 50.8 us
  Pallas kernels  47 us (92%)
  local copies, waits for them, and re-layouts  3.01 us (6%)
  between operations  0.75 us (1%)
    pallas_call x1, Pallas kernels, body(): pl.pallas_call(functools.partial(kernel, n_cell, n_inst, vpd), out_shape=...  47 us
    pallas_call x2, local copies, waits for them, and re-layouts, body(): pl.pallas_call(functools.partial(kernel, n_cell, n_inst, vpd), out_shape=...  1.71 us
    unnamed x15, local copies, waits for them, and re-layouts  1.31 us

profile of v1, /device:TPU:0, one launch (start us, length us, event | category | flops | bytes accessed | tf_op | source)
XLA Modules:
  0.0 50.8 jit_solution(1393516226847334574)
XLA Ops:
  0.6 0.0 copy-start
  0.6 0.0 copy-start.1
  0.7 0.0 copy-start.2
  0.7 0.0 copy-start.3
  0.7 0.0 copy-start.4
  0.7 0.0 copy-start.5
  0.7 0.0 copy-start.6
  0.7 1.3 %copy.10.fine_ref = f32[2,6,8192]{2,1,0:T(8,128)S(1)} copy(f32[2,6,8192]{2,0,1:T(2,128)} %param.8) | data formatting | bytes 786432 | tf_op args[0]
  2.0 0.0 copy-done
  2.0 0.0 copy-done.1
  2.0 0.0 copy-done.2
  2.0 0.0 copy-done.3
  2.0 0.0 copy-done.4
  2.0 0.0 copy-done.5
  2.0 0.0 copy-done.6
  2.0 47.0 %multigrid.1 = (f32[2,6,8192]{2,1,0:T(8,128)S(1)}, f32[2,6,1024]{2,1,0:T(8,128)S(1)}) custom-call(f32[2,6,8192]{2,1,0:T(8,128)S(1)} %copy.10.fine_ref, s32[1,8192]{1,0:T(1,128)S(1)} %bitcast.2, s32[1,64]{1,0:T(1,128)S(1)} %copy-done.6, s32[1,192]{1,0:T(1,128)S(1)} %copy-done.5, s32[6,1024]{1,0:T(8,128)S(1)} %copy-done.1, f32[6,1024]{1,0:T(8,128)S(1)} %copy-done.2, ...), custom_call_target="tpu_custom_call" | custom-call | tf_op jit(solution)/shard_map/multigrid/pallas_call | solution.py:297
  49.1 1.1 %copy.11 = f32[2,6,8192]{2,0,1:T(2,128)} copy(f32[2,6,8192]{2,1,0:T(8,128)S(1)} %get-tuple-element.2) | data formatting | bytes 786432 | tf_op jit(solution)/shard_map/multigrid/pallas_call | solution.py:297
  50.1 0.7 %copy.12 = f32[2,6,1024]{2,0,1:T(2,128)} copy(f32[2,6,1024]{2,1,0:T(8,128)S(1)} %get-tuple-element.3) | data formatting | bytes 98304 | tf_op jit(solution)/shard_map/multigrid/pallas_call | solution.py:297
Async XLA Ops:
  0.6 1.4 %copy-start = (s32[8192]{0:T(1024)S(1)}, s32[8192]{0:T(1024)}, u32[]{:S(2)}) copy-start(s32[8192]{0:T(1024)} %param.9) | copy-start | bytes 98308
  0.6 1.4 %copy-start.1 = (s32[6,1024]{1,0:T(8,128)S(1)}, s32[6,1024]{1,0:T(8,128)}, u32[]{:S(2)}) copy-start(s32[6,1024]{1,0:T(8,128)} %nb_ref.1) | copy-start | bytes 73732
  0.7 1.4 %copy-start.2 = (f32[6,1024]{1,0:T(8,128)S(1)}, f32[6,1024]{1,0:T(8,128)}, u32[]{:S(2)}) copy-start(f32[6,1024]{1,0:T(8,128)} %w_ref.1) | copy-start | bytes 73732
  0.7 1.4 %copy-start.3 = (f32[6,1024]{1,0:T(8,128)S(1)}, f32[6,1024]{1,0:T(8,128)}, u32[]{:S(2)}) copy-start(f32[6,1024]{1,0:T(8,128)} %de_ref.1) | copy-start | bytes 73732
  0.7 1.4 %copy-start.4 = (f32[1024]{0:T(1024)S(1)}, f32[1024]{0:T(1024)}, u32[]{:S(2)}) copy-start(f32[1024]{0:T(1024)} %param.14) | copy-start | bytes 12292
  0.7 1.4 %copy-start.5 = (s32[1,192]{1,0:T(1,128)S(1)}, s32[1,192]{1,0:T(1,128)}, u32[]{:S(2)}) copy-start(s32[1,192]{1,0:T(1,128)} %lists_ref.1) | copy-start | bytes 2308
  0.7 1.4 %copy-start.6 = (s32[1,64]{1,0:T(1,128)S(1)}, s32[1,64]{1,0:T(1,128)}, u32[]{:S(2)}) copy-start(s32[1,64]{1,0:T(1,128)} %routes_ref.1) | copy-start | bytes 772

commit v2 on v1

--- a/solution.py
+++ b/solution.py
@@ -65,16 +65,50 @@
     return jnp.where(part < 2, hi.astype(jnp.float32), lo.astype(jnp.float32)).astype(jnp.bfloat16)
 
 
+class Layout:
+    def __init__(self, n_cell, n_inst):
+        self.n_cell, self.n_inst = n_cell, n_inst
+        self.half = n_cell // 2
+        even = n_cell % 2 == 0 and n_inst % 2 == 0
+        self.folded = even and RAD < self.half <= 2 * RAD
+
+    def worker(self, part, group):
+        if not self.folded:
+            return part, group
+        wide = self.n_inst // 2
+        up, right = part >= self.half, group >= wide
+        cell = jnp.where(up, part - self.half, part) + jnp.where(right, self.half, 0)
+        return cell, 2 * jnp.where(right, group - wide, group) + jnp.where(up, 1, 0)
+
+    def role(self, cell, inst):
+        if not self.folded:
+            return cell, inst
+        up = cell >= self.half
+        core = lax.rem(inst, 2)
+        part = core * self.half + jnp.where(up, cell - self.half, cell)
+        return part, jnp.where(up, self.n_inst // 2, 0) + lax.div(inst, 2)
+
+    def served(self, inst):
+        if not self.folded:
+            return inst
+        return lax.div(inst, 2) + lax.rem(inst, 2) * (self.n_inst // 2)
+
+
+def wrap(value, count):
+    value = jnp.where(value >= count, value - count, value)
+    return jnp.where(value < 0, value + count, value)
+
+
 def kernel(
     n_cell, n_inst, vpd,
-    fine_ref, map_ref, routes_ref, lists_ref, nb_ref, w_ref, sc_ref, de_ref,
+    fine_ref, map_ref, routes_ref, lists_ref, nb_in, w_in, sc_in, de_in,
     fine_out, coarse_out,
-    e_ref, q_ref, ahi, alo, s_ref,
+    nb_ref, w_ref, sc_ref, de_ref, e_ref, q_ref, ahi, alo, s_ref,
     sbuf, rbuf, rlo, rhi, lbuf, obuf, hbuf, fbuf, gbuf, glo, ghi,
-    a_send, a_recv, l_send, l_recv, h_send, h_recv, f_send, f_recv,
+    w_send, w_recv, a_send, a_recv, l_send, l_recv, h_send, h_recv, f_send, f_recv,
 ):
     inst_dev, n_var, _ = fine_ref.shape
-    coarse = nb_ref.shape[1]
+    coarse = nb_in.shape[1]
     blocks = routes_ref.shape[1]
     hw = lists_ref.shape[1] // (2 * RAD)
     per = LANES // hw
@@ -88,17 +122,20 @@
     cell = lax.axis_index("cell")
     me = lax.axis_index("inst")
 
-    def at(dc, inst):
-        return {"cell": lax.rem(cell + (dc + n_cell), n_cell), "inst": inst}
-
-    def other(k):
-        return lax.rem(me + k, n_inst)
-
+    lay = Layout(n_cell, n_inst)
+    part, group = lay.role(cell, me)
+    devices = n_cell * n_inst
     barrier = pltpu.get_barrier_semaphore()
-    greeted = [(d, 0) for d in OFFSETS]
-    greeted += [(d, k) for d in (-1, 0, 1) for k in range(n_inst) if k]
-    for d, k in greeted:
-        pl.semaphore_signal(barrier, inc=1, device_id=at(d, other(k)), device_id_type=MESH)
+
+    def greet(k, carry):
+        for i in range(1 if isinstance(k, int) else 0, n_inst):
+            pl.semaphore_signal(
+                barrier, inc=1, device_id_type=MESH,
+                device_id={"cell": wrap(cell + k, n_cell), "inst": wrap(me + i, n_inst)})
+        return carry
+
+    greet(0, 0)
+    lax.fori_loop(1, n_cell, greet, 0)
 
     lane = iota((1, span), 1)
     sub = iota((LANES, span), 0)
@@ -107,14 +144,54 @@
         want = map_ref[:, g * span:(g + 1) * span] + (lane // BLK) * CBLK
         e_ref[g] = as_bf16(sub == want)
         x = fine_ref[:, :, g * span:(g + 1) * span]
-        pieces = []
-        for i in range(inst_dev):
-            pieces.append(x[i])
-            if pad_var > n_var:
-                pieces.append(jnp.zeros((pad_var - n_var, span), jnp.float32))
+        pieces = [x[i, v:v + 1] for v in range(n_var) for i in range(inst_dev)]
+        if pad_var > n_var:
+            pieces.append(jnp.zeros(((pad_var - n_var) * inst_dev, span), jnp.float32))
         x = jnp.concatenate(pieces, axis=0)
         parts.append(fold(dot(stack(x), e_ref[g], NT)))
     y = jnp.concatenate(parts, axis=1)
+
+    def remote(src, dst, send, recv, where):
+        return pltpu.make_async_remote_copy(
+            src_ref=src, dst_ref=dst, send_sem=send, recv_sem=recv,
+            device_id={"cell": where[0], "inst": where[1]}, device_id_type=MESH)
+
+    def away(where, then):
+        pl.when((where[0] != cell) | (where[1] != me))(then)
+
+    def home(where, then):
+        pl.when((where[0] == cell) & (where[1] == me))(then)
+
+    def near(p, d):
+        return wrap(p + d, n_cell)
+
+    def swap(src, mid, low, high, send, recv, slot, target, dc, source):
+        first, last = pl.ds(0, LANES), pl.ds(coarse - LANES, LANES)
+        for k in range(n_inst):
+            where = target(0, k)
+            copy = remote(src.at[k], mid.at[slot], send.at[0, k], recv.at[0, slot], where)
+            away(where, copy.start)
+
+            def keep():
+                mid[slot] = src[k]
+
+            home(where, keep)
+            remote(src.at[k, :, first], low.at[slot], send.at[1, k], recv.at[1, slot],
+                   target(dc, k)).start()
+            remote(src.at[k, :, last], high.at[slot], send.at[2, k], recv.at[2, slot],
+                   target(-dc, k)).start()
+
+        def finish():
+            for k in range(n_inst):
+                arrival = remote(src.at[k], mid.at[k], send.at[0, k], recv.at[0, k], source(k))
+                away(source(k), arrival.wait_recv)
+                away(target(0, k), arrival.wait_send)
+                remote(src.at[k, :, first], low.at[k], send.at[1, k], recv.at[1, k],
+                       target(dc, k)).wait()
+                remote(src.at[k, :, last], high.at[k], send.at[2, k], recv.at[2, k],
+                       target(-dc, k)).wait()
+
+        return finish
 
     rel = lax.rem(routes_ref[...] - cell + n_cell, n_cell)
     kinds = [(rel == 1), (rel == 0), (rel != 1) & (rel != 0)]
@@ -131,44 +208,58 @@
     target = pos.astype(jnp.int32) * CBLK + iota((1, coarse), 1) % CBLK
     q_ref[...] = as_bf16(iota((coarse, coarse), 0) == target)
 
+    pl.semaphore_wait(barrier, devices - 1)
+
+    mine = lay.served(me)
+    weights = [(nb_in, nb_ref), (w_in, w_ref), (sc_in, sc_ref), (de_in, de_ref)]
+    if lay.folded:
+        goal = lay.worker(cell, mine)
+        weight_copies = [
+            remote(src, dst, w_send.at[n], w_recv.at[n], goal)
+            for n, (src, dst) in enumerate(weights)]
+
+        def send_weights():
+            for copy in weight_copies:
+                copy.start()
+
+        def keep_weights():
+            for src, dst in weights:
+                dst[...] = src[...]
+
+        away(goal, send_weights)
+        home(goal, keep_weights)
+    else:
+        for src, dst in weights:
+            dst[...] = src[...]
+
+    list_copies = [
+        remote(lists_ref, lbuf.at[t], l_send.at[t], l_recv.at[t],
+               lay.worker(near(cell, OFFSETS[t]), mine))
+        for t in range(2 * RAD)]
+    for copy in list_copies:
+        copy.start()
+
     row = iota((inst_dev * pad_var, 1), 0)
-    live = me * inst_dev + row // pad_var < HB_INST
+    live = me * inst_dev + row % inst_dev < HB_INST
     y = jnp.where(live, fold(dot(stack(y), q_ref[...], NT)), 0.0)
+    width = vpd * inst_dev
     for j in range(n_inst):
-        picked = []
-        for v in range(vpd):
-            for i in range(inst_dev):
-                r = i * pad_var + j * vpd + v
-                picked.append(y[r:r + 1])
-        sbuf[j] = jnp.concatenate(picked, axis=0)
-
-    pl.semaphore_wait(barrier, len(greeted))
-
-    def remote(src, dst, send, recv, dc, inst):
-        copy = pltpu.make_async_remote_copy(
-            src_ref=src, dst_ref=dst, send_sem=send, recv_sem=recv,
-            device_id=at(dc, inst), device_id_type=MESH)
-        copy.start()
-        return copy
-
-    def swap(src, mid, low, high, send, recv, dc):
-        copies = []
-        for k in range(n_inst):
-            j = other(k)
-            if k:
-                copies.append(remote(src.at[j], mid.at[me], send.at[0, k], recv.at[0, k], 0, j))
-            copies.append(remote(
-                src.at[j, :, pl.ds(0, LANES)], low.at[me], send.at[1, k], recv.at[1, k], dc, j))
-            copies.append(remote(
-                src.at[j, :, pl.ds(coarse - LANES, LANES)], high.at[me],
-                send.at[2, k], recv.at[2, k], -dc, j))
-        mid[me] = src[me]
-        return copies
-
-    list_copies = [
-        remote(lists_ref, lbuf.at[t], l_send.at[t], l_recv.at[t], OFFSETS[t], me)
-        for t in range(2 * RAD)]
-    swaps = swap(sbuf, rbuf, rlo, rhi, a_send, a_recv, 1)
+        sbuf[j] = y[j * width:(j + 1) * width]
+    arrive = swap(sbuf, rbuf, rlo, rhi, a_send, a_recv, me,
+                  lambda d, k: lay.worker(near(cell, d), k), 1, lambda k: (part, k))
+
+    if lay.folded:
+        def take_weights():
+            for copy in weight_copies:
+                copy.wait_recv()
+
+        def sent_weights():
+            for copy in weight_copies:
+                copy.wait_send()
+
+        origin = (part, lax.div(me, 2) * 2 + jnp.where(cell >= lay.half, 1, 0))
+        away(origin, take_weights)
+        away(goal, sent_weights)
 
     chunk = 64
 
@@ -191,7 +282,7 @@
     for v in range(vpd):
         extra = jnp.zeros_like(sc)
         for var in range(n_var):
-            extra = jnp.where(me * vpd + v == var, de_ref[var:var + 1], extra)
+            extra = jnp.where(group * vpd + v == var, de_ref[var:var + 1], extra)
         diags.append(jnp.broadcast_to(wsum + extra, (INST, coarse)))
     rinv = 1.0 / jnp.concatenate(diags, axis=0)
     scr = sc * rinv
@@ -219,8 +310,7 @@
                 [value[:, start:], jnp.zeros((1, start + LANES - width), jnp.int32)], axis=1)
         s_ref[:, tile * LANES:(tile + 1) * LANES] = as_bf16(sub == pick(tile, listed))
 
-    for copy in swaps:
-        copy.wait()
+    arrive()
     wide = iota((1, coarse), 1)
 
     def edges(whole, low, high):
@@ -235,6 +325,8 @@
             axis=0)
 
     first = edges(ordered(rbuf), ordered(rlo), ordered(rhi)) * rinv
+
+    peers = [lay.worker(near(part, -d), group) for d in OFFSETS]
 
     def sweep(s, x):
         hi, lo = split(x)
@@ -244,8 +336,10 @@
             obuf[s, tile] = out[:, tile * LANES:(tile + 1) * LANES]
         copies = [
             remote(obuf.at[s, t // per], hbuf.at[s, t], h_send.at[s, t], h_recv.at[s, t],
-                   -OFFSETS[t], me)
+                   peers[t])
             for t in range(2 * RAD)]
+        for copy in copies:
+            copy.start()
         total = fold(dot(both, ahi[:coarse])) + dot(hi, alo[:coarse])
         coupled = dot(spec, jnp.concatenate([hi, lo, hi], axis=0))
         partial = first + total * rinv - coupled * scr
@@ -262,23 +356,24 @@
     for i in range(n_inst):
         fbuf[i] = jnp.concatenate(
             [x[v * INST + i * inst_dev:v * INST + (i + 1) * inst_dev] for v in range(vpd)], axis=0)
-    swaps = swap(fbuf, gbuf, glo, ghi, f_send, f_recv, -1)
-    for copy in swaps:
-        copy.wait()
+    arrive = swap(fbuf, gbuf, glo, ghi, f_send, f_recv, group,
+                  lambda d, k: (near(part, d), k), -1, lambda k: lay.worker(cell, k))
+    arrive()
 
     def by_var(buf):
-        return jnp.concatenate(
-            [buf[j, v * inst_dev + i:v * inst_dev + i + 1]
-             for i in range(inst_dev) for j in range(n_inst) for v in range(vpd)], axis=0)
+        return jnp.concatenate([buf[j] for j in range(n_inst)], axis=0)
 
     whole = by_var(gbuf)
-    for i in range(inst_dev):
-        coarse_out[i] = whole[i * pad_var:i * pad_var + n_var]
+    for v in range(n_var):
+        for i in range(inst_dev):
+            coarse_out[i, v:v + 1] = whole[v * inst_dev + i:v * inst_dev + i + 1]
     back = dot(stack(edges(whole, by_var(glo), by_var(ghi))), q_ref[...]).astype(jnp.bfloat16)
     for g in range(groups):
         fine = fold(dot(back[:, g * LANES:(g + 1) * LANES], e_ref[g]))
-        for i in range(inst_dev):
-            fine_out[i, :, g * span:(g + 1) * span] = fine[i * pad_var:i * pad_var + n_var]
+        for v in range(n_var):
+            for i in range(inst_dev):
+                r = v * inst_dev + i
+                fine_out[i, v:v + 1, g * span:(g + 1) * span] = fine[r:r + 1]
 
 
 def body(n_cell, n_inst, fine_residual, fine_map, routes, receive_lists, neighbours,
@@ -294,7 +389,7 @@
     f32, bf16 = jnp.float32, jnp.bfloat16
     vmem = pl.BlockSpec(memory_space=pltpu.VMEM)
     dma = pltpu.SemaphoreType.DMA
-    return pl.pallas_call(
+    fine_correction, correction = pl.pallas_call(
         functools.partial(kernel, n_cell, n_inst, vpd),
         out_shape=(
             jax.ShapeDtypeStruct(fine_residual.shape, f32),
@@ -303,6 +398,10 @@
         in_specs=[vmem] * 8,
         out_specs=(vmem, vmem),
         scratch_shapes=[
+            pltpu.VMEM(neighbours.shape, jnp.int32),
+            pltpu.VMEM(face_weights.shape, f32),
+            pltpu.VMEM((1, coarse), f32),
+            pltpu.VMEM(diag_extra.shape, f32),
             pltpu.VMEM((blocks // PER_TILE, LANES, PER_TILE * BLK), bf16),
             pltpu.VMEM((coarse, coarse), bf16),
             pltpu.VMEM((coarse + n_halo, coarse), bf16),
@@ -319,6 +418,7 @@
             pltpu.VMEM((n_inst, part, coarse), f32),
             pltpu.VMEM((n_inst, part, LANES), f32),
             pltpu.VMEM((n_inst, part, LANES), f32),
+            dma((4,)), dma((4,)),
             dma((3, n_inst)), dma((3, n_inst)),
             dma((2 * RAD,)), dma((2 * RAD,)),
             dma((ITERS, 2 * RAD)), dma((ITERS, 2 * RAD)),
@@ -329,6 +429,7 @@
         name="multigrid",
     )(fine_residual, fine_map.reshape(1, -1), routes, receive_lists, neighbours,
       face_weights, spectral_coef.reshape(1, -1), diag_extra)
+    return fine_correction, correction
 
 
 def solution(mesh):

time: 50.9 us -> 48.8 us (0.959)
  Pallas kernels: 47 us -> 44.9 us
    pallas_call x1, Pallas kernels: 47 us -> 44.9 us  [body(): pl.pallas_call(functools.partial(kernel, n_cell, n_inst, vpd), out_shape=...]
where the time goes in v2:
time: 48.8 us; the launch traced here: 48.7 us
  Pallas kernels  44.9 us (92%)
  local copies, waits for them, and re-layouts  3.01 us (6%)
  between operations  0.75 us (2%)
    pallas_call x1, Pallas kernels, body(): pl.pallas_call(functools.partial(kernel, n_cell, n_inst, vpd), out_shape=...  44.9 us
    pallas_call x2, local copies, waits for them, and re-layouts, body(): pl.pallas_call(functools.partial(kernel, n_cell, n_inst, vpd), out_shape=...  1.71 us
    unnamed x15, local copies, waits for them, and re-layouts  1.31 us

profile of v2, /device:TPU:0, one launch (start us, length us, event | category | flops | bytes accessed | tf_op | source)
XLA Modules:
  0.0 48.7 jit_solution(15332243151601627790)
XLA Ops:
  0.6 0.0 copy-start
  0.6 0.0 copy-start.1
  0.7 0.0 copy-start.2
  0.7 0.0 copy-start.3
  0.7 0.0 copy-start.4
  0.7 0.0 copy-start.5
  0.7 0.0 copy-start.6
  0.7 1.3 %copy.10.fine_ref = f32[2,6,8192]{2,1,0:T(8,128)S(1)} copy(f32[2,6,8192]{2,0,1:T(2,128)} %param.8) | data formatting | bytes 786432 | tf_op args[0]
  2.0 0.0 copy-done
  2.0 0.0 copy-done.1
  2.0 0.0 copy-done.2
  2.0 0.0 copy-done.3
  2.0 0.0 copy-done.4
  2.0 0.0 copy-done.5
  2.0 0.0 copy-done.6
  2.0 44.9 %multigrid.1 = (f32[2,6,8192]{2,1,0:T(8,128)S(1)}, f32[2,6,1024]{2,1,0:T(8,128)S(1)}) custom-call(f32[2,6,8192]{2,1,0:T(8,128)S(1)} %copy.10.fine_ref, s32[1,8192]{1,0:T(1,128)S(1)} %bitcast.2, s32[1,64]{1,0:T(1,128)S(1)} %copy-done.6, s32[1,192]{1,0:T(1,128)S(1)} %copy-done.5, s32[6,1024]{1,0:T(8,128)S(1)} %copy-done.1, f32[6,1024]{1,0:T(8,128)S(1)} %copy-done.2, ...), custom_call_target="tpu_custom_call" | custom-call | tf_op jit(solution)/shard_map/multigrid/pallas_call | solution.py:392
  47.0 1.1 %copy.11 = f32[2,6,8192]{2,0,1:T(2,128)} copy(f32[2,6,8192]{2,1,0:T(8,128)S(1)} %get-tuple-element.2) | data formatting | bytes 786432 | tf_op jit(solution)/shard_map/multigrid/pallas_call | solution.py:392
  48.0 0.7 %copy.12 = f32[2,6,1024]{2,0,1:T(2,128)} copy(f32[2,6,1024]{2,1,0:T(8,128)S(1)} %get-tuple-element.3) | data formatting | bytes 98304 | tf_op jit(solution)/shard_map/multigrid/pallas_call | solution.py:392
Async XLA Ops:
  0.6 1.4 %copy-start = (s32[8192]{0:T(1024)S(1)}, s32[8192]{0:T(1024)}, u32[]{:S(2)}) copy-start(s32[8192]{0:T(1024)} %param.9) | copy-start | bytes 98308
  0.6 1.4 %copy-start.1 = (s32[6,1024]{1,0:T(8,128)S(1)}, s32[6,1024]{1,0:T(8,128)}, u32[]{:S(2)}) copy-start(s32[6,1024]{1,0:T(8,128)} %nb_in.1) | copy-start | bytes 73732
  0.7 1.4 %copy-start.2 = (f32[6,1024]{1,0:T(8,128)S(1)}, f32[6,1024]{1,0:T(8,128)}, u32[]{:S(2)}) copy-start(f32[6,1024]{1,0:T(8,128)} %w_in.1) | copy-start | bytes 73732
  0.7 1.4 %copy-start.3 = (f32[6,1024]{1,0:T(8,128)S(1)}, f32[6,1024]{1,0:T(8,128)}, u32[]{:S(2)}) copy-start(f32[6,1024]{1,0:T(8,128)} %de_in.1) | copy-start | bytes 73732
  0.7 1.4 %copy-start.4 = (f32[1024]{0:T(1024)S(1)}, f32[1024]{0:T(1024)}, u32[]{:S(2)}) copy-start(f32[1024]{0:T(1024)} %param.14) | copy-start | bytes 12292
  0.7 1.4 %copy-start.5 = (s32[1,192]{1,0:T(1,128)S(1)}, s32[1,192]{1,0:T(1,128)}, u32[]{:S(2)}) copy-start(s32[1,192]{1,0:T(1,128)} %lists_ref.1) | copy-start | bytes 2308
  0.7 1.4 %copy-start.6 = (s32[1,64]{1,0:T(1,128)S(1)}, s32[1,64]{1,0:T(1,128)}, u32[]{:S(2)}) copy-start(s32[1,64]{1,0:T(1,128)} %routes_ref.1) | copy-start | bytes 772
